TPU v7x, 32 devices: a whole 2x2x4 slice. The times are simulated.
32 devices in a mesh: col: 16 (over z, y, x), row: 2 (over core).
Axes of the slice: x: 2, y: 2, z: 4, core: 2. Of those that a mesh axis runs over, the one named last changes fastest.
Arguments:
- kernel: float32 [512, 131072], P('row', 'col'), may hold values from -0.0234375 to 0.0234375
- slip_deficit: float32 [64, 131072], P(None, ('col', 'row')), may hold values from -6 to 6
- loading: float32 [512], P('row'), may hold values from -4 to 4
- direct_effect: float32 [512], P('row'), may hold values from 1 to 4
- log_state: float32 [64, 512], P(None, 'row'), may hold values from -1 to 1
Outputs:
- slip_rate: float32 [64, 512], P(None, 'row')
- next_state: float32 [64, 512], P(None, 'row')
All inputs are finite; a program needn't handle non-finite values. Where the computation divides by a largest or mean magnitude, that divisor is 1e-20 or more.
Results may differ from a plain program's by a relative error of at most 0.00013.
Values sent between devices are 32-bit elements; how exact they have to be, the bound alone decides.
A program may use at most 64 MiB of HBM per device.

v0:
```python
import jax
import jax.numpy as jnp
from jax import lax
from jax.sharding import PartitionSpec as P


def friction(stress, direct_effect, log_state):
    return 2.0 * jnp.exp(-log_state) * jnp.sinh(stress / direct_effect[None, :])


def evolve(log_state, slip_rate, peak_rate):
    step_size = 1.0 / (peak_rate + 1e-06)
    return log_state + step_size[:, None] * (jnp.exp(-log_state) - jnp.abs(slip_rate))


def on_device(kernel, slip_deficit, loading, direct_effect, log_state):
    partial_stress = lax.dot_general(
        lax.all_gather(slip_deficit, "row", axis=1, tiled=True),
        kernel,
        (((1,), (1,)), ((), ())),
        precision=lax.Precision.HIGHEST,
        preferred_element_type=jnp.float32,
    )
    stress = lax.psum(partial_stress, "col") + loading[None, :]
    slip_rate = friction(stress, direct_effect, log_state)
    peak_rate = lax.pmax(jnp.max(jnp.abs(slip_rate), axis=1), "row")
    next_state = evolve(log_state, slip_rate, peak_rate)
    return (slip_rate, next_state)


def solution(mesh):
    return jax.shard_map(
        on_device,
        mesh=mesh,
        in_specs=(P("row", "col"), P(None, ("col", "row")), P("row"), P("row"), P(None, "row")),
        out_specs=(P(None, "row"), P(None, "row")),
        check_vma=False,
    )
```

profile of v0, /device:TPU:0, one launch (start us, length us, event | category | flops | bytes accessed | tf_op | source)
XLA Modules:
  0.0 151.2 jit_solution(1238443934083582144)
XLA Ops:
  7.2 0.0 copy-start
  7.2 0.0 copy-start.2
  7.2 0.0 copy-start.3
  7.2 0.0 all-gather.2.cloned.1.call-start
  7.2 0.7 all-gather.2.cloned.1.call-update
  7.9 0.0 all-reduce.2.cloned.1.call-start
  8.0 14.9 %all-gather.2.cloned.1.call-done = f32[64,8192]{1,0:T(8,128)} async-done(((f32[64,4096]{1,0:T(8,128)}), f32[64,8192]{1,0:T(8,128)}) %all-gather.2.cloned.1.call-update) | async-done | bytes 2097168 | tf_op jit(solution)/shard_map/all_gather | solution.py:18
  22.9 12.4 %fusion.4 = f32[64,256]{1,0:T(8,128)} fusion(f32[64,8192]{1,0:T(8,128)} %all-gather.2.cloned.1.call-done, f32[256,8192]{1,0:T(8,128)} %param.5), kind=kOutput, calls=%fused_computation.9 | convolution fusion | flops 1610612736 | bytes 10551296 | tf_op jit(solution)/shard_map/dot_general | solution.py:17
  35.3 0.0 all-reduce.2.cloned.1.call-update
  35.3 104.8 %all-reduce.2.cloned.1.call-done = f32[64,256]{1,0:T(8,128)} async-done(((f32[64,256]{1,0:T(8,128)}), f32[64,256]{1,0:T(8,128)}) %all-reduce.2.cloned.1.call-update) | async-done | bytes 65552 | tf_op jit(solution)/shard_map/psum | solution.py:24
  140.1 0.0 copy-done
  140.1 0.0 copy-done.2
  140.1 0.0 copy-done.3
  140.1 1.0 abs_reduce_fusion
  141.1 0.0 copy-start.1
  141.1 2.5 %pmax.7 = f32[64]{0:T(128)S(1)} all-reduce(f32[64]{0:T(128)S(1)} %get-tuple-element.2), channel_id=1, replica_groups=mesh['col'=16,'row'=2] {'row'}, use_global_device_ids=true, to_apply=%region_2.0 | all-reduce | flops 64 | bytes 512 | tf_op jit(solution)/shard_map/pmax | solution.py:26
  143.6 0.7 multiply_add_fusion
  144.3 0.0 copy-done.1
  (1 shorter events, 0.0 us)
Async XLA Ops:
  7.2 132.9 %copy-start = (f32[64,256]{1,0:T(8,128)S(1)}, f32[64,256]{1,0:T(8,128)}, u32[]{:S(2)}) copy-start(f32[64,256]{1,0:T(8,128)} %param.9) | copy-start | bytes 196612
  7.2 132.9 %copy-start.2 = (f32[256]{0:T(256)S(1)}, f32[256]{0:T(256)}, u32[]{:S(2)}) copy-start(f32[256]{0:T(256)} %param.8) | copy-start | bytes 3076
  7.2 132.9 %copy-start.3 = (f32[256]{0:T(256)S(1)}, f32[256]{0:T(256)}, u32[]{:S(2)}) copy-start(f32[256]{0:T(256)} %param.7) | copy-start | bytes 3076
  7.2 15.7 %all-gather.2.cloned.1.call-start = ((), (), s32[]{:S(2)}) async-start(), calls=%async_computation | async-start | bytes 3145728 | tf_op jit(solution)/shard_map/all_gather | solution.py:18
  7.9 132.2 %all-reduce.2.cloned.1.call-start = ((), (), s32[]{:S(2)}) async-start(), calls=%async_computation.1 | async-start | bytes 131072 | tf_op jit(solution)/shard_map/psum | solution.py:24
  141.1 3.2 %copy-start.1 = (f32[64,256]{1,0:T(8,128)}, f32[64,256]{1,0:T(8,128)S(1)}, u32[]{:S(2)}) copy-start(f32[64,256]{1,0:T(8,128)S(1)} %get-tuple-element.3) | copy-start | bytes 196612
Sparse Core Ops, SparseCore 0:
  9.5 13.2 all-gather.1
  35.4 104.6 all-reduce.1
where the time goes:
time: 151 us
  waiting for transfers between devices  120 us (79%)
  between operations  14.1 us (9%)
  matrix products  12.4 us (8%)
  blocking collectives  2.47 us (2%)
  other arithmetic  1.74 us (1%)
    psum x1, waiting for transfers between devices, on_device(): stress = lax.psum(partial_stress, 'col') + loading[None, :]  105 us
    all_gather x1, waiting for transfers between devices, on_device(): lax.all_gather(slip_deficit, 'row', axis=1, tiled=True)  14.9 us
    dot_general x1, matrix products, on_device(): lax.dot_general(lax.all_gather(slip_deficit, 'row', axis=1, tiled=True),...  12.4 us
  transfers between devices with their start and end apart: 2, of which 2 were waited for; matrix products, arithmetic and copies ran while one was open for 0% of the time, Pallas kernels for 0%

commit v1 on v0

--- a/solution.py
+++ b/solution.py
@@ -21,7 +21,7 @@
         precision=lax.Precision.HIGHEST,
         preferred_element_type=jnp.float32,
     )
-    stress = lax.psum(partial_stress, "col") + loading[None, :]
+    stress = jnp.sum(lax.all_gather(partial_stress, "col"), axis=0) + loading[None, :]
     slip_rate = friction(stress, direct_effect, log_state)
     peak_rate = lax.pmax(jnp.max(jnp.abs(slip_rate), axis=1), "row")
     next_state = evolve(log_state, slip_rate, peak_rate)

time: 151 us -> 103 us (0.68)
  waiting for transfers between devices: 120 us -> 72 us
    psum x1 -> x0, waiting for transfers between devices: 105 us -> none  [on_device(): stress = lax.psum(partial_stress, 'col') + loading[None, :]]
    all_gather x0 -> x1, waiting for transfers between devices: none -> 56.4 us  [on_device(): lax.all_gather(partial_stress, 'col')]
where the time goes in v1:
time: 103 us
  waiting for transfers between devices  72 us (70%)
  between operations  14.1 us (14%)
  matrix products  12.4 us (12%)
  blocking collectives  2.47 us (2%)
  other arithmetic  2.19 us (2%)
    all_gather x1, waiting for transfers between devices, on_device(): lax.all_gather(partial_stress, 'col')  56.4 us
    all_gather x1, waiting for transfers between devices, on_device(): lax.all_gather(slip_deficit, 'row', axis=1, tiled=True)  14.9 us
    dot_general x1, matrix products, on_device(): lax.dot_general(lax.all_gather(slip_deficit, 'row', axis=1, tiled=True),...  12.4 us
    pmax x1, blocking collectives, on_device(): peak_rate = lax.pmax(jnp.max(jnp.abs(slip_rate), axis=1), 'row')  2.47 us
  transfers between devices with their start and end apart: 2, of which 2 were waited for; matrix products, arithmetic and copies ran while one was open for 0% of the time, Pallas kernels for 0%

profile of v1, /device:TPU:0, one launch (start us, length us, event | category | flops | bytes accessed | tf_op | source)
XLA Modules:
  0.0 103.3 jit_solution(16969161462528607178)
XLA Ops:
  7.2 0.0 copy-start
  7.2 0.0 copy-start.2
  7.2 0.0 copy-start.3
  7.2 0.0 all-gather.4.cloned.1.call-start
  7.2 0.7 all-gather.4.cloned.1.call-update
  7.9 0.0 all-gather.6.cloned.1.call-start
  8.0 14.9 %all-gather.4.cloned.1.call-done = f32[64,8192]{1,0:T(8,128)} async-done(((f32[64,4096]{1,0:T(8,128)}), f32[64,8192]{1,0:T(8,128)}) %all-gather.4.cloned.1.call-update) | async-done | bytes 2097168 | tf_op jit(solution)/shard_map/all_gather | solution.py:18
  22.9 12.4 %fusion.4 = f32[64,256]{1,0:T(8,128)} fusion(f32[64,8192]{1,0:T(8,128)} %all-gather.4.cloned.1.call-done, f32[256,8192]{1,0:T(8,128)} %param.5), kind=kOutput, calls=%fused_computation.9 | convolution fusion | flops 1610612736 | bytes 10551296 | tf_op jit(solution)/shard_map/dot_general | solution.py:17
  35.3 0.0 all-gather.6.cloned.1.call-update
  35.3 56.4 %all-gather.6.cloned.1.call-done = f32[1024,256]{1,0:T(8,128)} async-done(((f32[64,256]{1,0:T(8,128)}), f32[1024,256]{1,0:T(8,128)}) %all-gather.6.cloned.1.call-update) | async-done | bytes 1048592 | tf_op jit(solution)/shard_map/all_gather | solution.py:24
  91.7 1.3 %reduce_sum.9 = f32[64,256]{1,0:T(8,128)S(1)} reduce(f32[16,64,256]{2,1,0:T(8,128)} %bitcast.3, f32[]{:T(128)} %constant.0.clone.1), dimensions={0}, to_apply=%region_0.0 | reduce | flops 245760 | bytes 1114116 | tf_op jit(solution)/shard_map/reduce_sum | solution.py:24
  93.0 0.0 copy-done
  93.0 0.0 copy-done.2
  93.0 0.0 copy-done.3
  93.0 0.2 abs_reduce_fusion
  93.2 0.0 copy-start.1
  93.2 2.5 %pmax.7 = f32[64]{0:T(128)S(1)} all-reduce(f32[64]{0:T(128)S(1)} %get-tuple-element.2), channel_id=1, replica_groups=mesh['col'=16,'row'=2] {'row'}, use_global_device_ids=true, to_apply=%region_2.0 | all-reduce | flops 64 | bytes 512 | tf_op jit(solution)/shard_map/pmax | solution.py:26
  95.7 0.7 multiply_add_fusion
  96.4 0.0 copy-done.1
  (1 shorter events, 0.0 us)
Async XLA Ops:
  7.2 85.9 %copy-start = (f32[64,256]{1,0:T(8,128)S(1)}, f32[64,256]{1,0:T(8,128)}, u32[]{:S(2)}) copy-start(f32[64,256]{1,0:T(8,128)} %param.9) | copy-start | bytes 196612
  7.2 85.9 %copy-start.2 = (f32[256]{0:T(256)S(1)}, f32[256]{0:T(256)}, u32[]{:S(2)}) copy-start(f32[256]{0:T(256)} %param.8) | copy-start | bytes 3076
  7.2 85.9 %copy-start.3 = (f32[256]{0:T(256)S(1)}, f32[256]{0:T(256)}, u32[]{:S(2)}) copy-start(f32[256]{0:T(256)} %param.7) | copy-start | bytes 3076
  7.2 15.7 %all-gather.4.cloned.1.call-start = ((), (), s32[]{:S(2)}) async-start(), calls=%async_computation | async-start | bytes 3145728 | tf_op jit(solution)/shard_map/all_gather | solution.py:18
  7.9 83.8 %all-gather.6.cloned.1.call-start = ((), (), s32[]{:S(2)}) async-start(), calls=%async_computation.1 | async-start | bytes 1114112 | tf_op jit(solution)/shard_map/all_gather | solution.py:24
  93.2 3.2 %copy-start.1 = (f32[64,256]{1,0:T(8,128)}, f32[64,256]{1,0:T(8,128)S(1)}, u32[]{:S(2)}) copy-start(f32[64,256]{1,0:T(8,128)S(1)} %get-tuple-element.3) | copy-start | bytes 196612
Sparse Core Ops, SparseCore 0:
  9.5 13.2 all-gather.3
  35.4 56.2 all-gather.5
